TPU v7x, 256 devices: a whole 4x4x8 slice. The times are simulated.
256 devices in a mesh: row: 32 (over y, z), col: 8 (over x, core).
Axes of the slice: x: 4, y: 4, z: 8, core: 2. Of those that a mesh axis runs over, the one named last changes fastest.
Arguments:
- features: bfloat16 [49152, 4096], P(('row', 'col')), may hold values from -24 to 24
- cotangent: bfloat16 [49152, 8192], P(('row', 'col')), may hold values from -0.02734375 to 0.02734375
Outputs:
- weight_grad: float32 [4096, 8192], P('row', 'col')
All inputs are finite; a program needn't handle non-finite values.
Results may differ from a plain program's by a relative error of at most 0.0003.
Values may be sent and summed in bfloat16 or wider, within the bound.
A program may use at most 256 MiB of HBM per device.

v0:
```python
import jax
import jax.numpy as jnp
from jax import lax
from jax.sharding import Mesh
from jax.sharding import PartitionSpec as P

ROW = ("row_0", "row_1")
ROW_COL = ("row_0", "row_1", "col")


def sum_by_axis(array, axes, dim):
    for axis in axes:
        array = lax.psum_scatter(array, axis, scatter_dimension=dim, tiled=True)
    return array


def tokens_product(left, right):
    return lax.dot_general(
        left, right, (((0,), (0,)), ((), ())), preferred_element_type=jnp.float32
    )


def local(features, cotangent):
    columns = lax.all_to_all(cotangent, "col", split_axis=1, concat_axis=0, tiled=True)
    partial_value = tokens_product(lax.all_gather(features, "col", axis=0, tiled=True), columns)
    return sum_by_axis(partial_value, ROW, 0)


def solution(mesh):
    torus = Mesh(mesh.devices.reshape(4, 8, mesh.shape["col"]), ("row_0", "row_1", "col"))
    in_specs = (P(ROW_COL, None), P(ROW_COL, None))
    out_specs = P(ROW, "col")
    return jax.shard_map(local, mesh=torus, in_specs=in_specs, out_specs=out_specs, check_vma=False)
```

profile of v0, /device:TPU:1, one launch (start us, length us, event | category | flops | bytes accessed | tf_op | source)
XLA Modules:
  0.0 340.8 jit_solution(15472205882023542649)
XLA Ops:
  6.5 0.0 all-gather.2.cloned.1.call-start
  6.5 0.7 all-gather.2.cloned.1.call-update
  7.3 0.0 reduce-scatter.3.cloned.1.call-start
  7.3 2.3 copy.7
  9.6 65.5 %all_to_all.19 = bf16[192,8,1024]{2,0,1:T(8,128)(2,1)S(1)} all-to-all(bf16[192,8,1024]{2,0,1:T(8,128)(2,1)S(1)} %bitcast.9), channel_id=1, replica_groups=mesh['row_0'=4,'row_1'=8,'col'=8] {'col'}, dimensions={1} | all-to-all | bytes 6291456 | tf_op jit(solution)/shard_map/all_to_all | solution.py:24
  75.1 30.6 %all-gather.2.cloned.1.call-done = bf16[1536,4096]{1,0:T(8,128)(2,1)} async-done(((bf16[192,4096]{1,0:T(8,128)(2,1)}), bf16[1536,4096]{1,0:T(8,128)(2,1)}) %all-gather.2.cloned.1.call-update) | async-done | bytes 12582928 | tf_op jit(solution)/shard_map/all_gather | solution.py:25
  105.7 19.5 %fusion = f32[4096,1024]{1,0:T(8,128)} fusion(bf16[1536,4096]{1,0:T(8,128)(2,1)} %all-gather.2.cloned.1.call-done, bf16[1536,1024]{1,0:T(8,128)(2,1)S(1)} %bitcast.11), kind=kOutput, calls=%fused_computation.1 | convolution fusion | flops 12884901888 | bytes 32505856 | tf_op jit(solution)/shard_map/dot_general | solution.py:18
  125.2 0.0 reduce-scatter.3.cloned.1.call-update
  125.3 0.0 reduce-scatter.5.cloned.1.call-start
  125.3 151.3 %reduce-scatter.3.cloned.1.call-done = f32[1024,1024]{1,0:T(8,128)} async-done(((f32[4096,1024]{1,0:T(8,128)}), f32[1024,1024]{1,0:T(8,128)}) %reduce-scatter.3.cloned.1.call-update) | async-done | bytes 4194320 | tf_op jit(solution)/shard_map/reduce_scatter | solution.py:13
  276.6 0.0 reduce-scatter.5.cloned.1.call-update
  276.6 57.6 %reduce-scatter.5.cloned.1.call-done = f32[128,1024]{1,0:T(8,128)} async-done(((f32[1024,1024]{1,0:T(8,128)}), f32[128,1024]{1,0:T(8,128)}) %reduce-scatter.5.cloned.1.call-update) | async-done | bytes 524304 | tf_op jit(solution)/shard_map/reduce_scatter | solution.py:13
Async XLA Ops:
  6.5 99.2 %all-gather.2.cloned.1.call-start = ((), (), s32[]{:S(2)}) async-start(), calls=%async_computation.3 | async-start | bytes 14155776 | tf_op jit(solution)/shard_map/all_gather | solution.py:25
  7.3 269.4 %reduce-scatter.3.cloned.1.call-start = ((), (), s32[]{:S(2)}) async-start(), calls=%async_computation.4 | async-start | bytes 20971520 | tf_op jit(solution)/shard_map/reduce_scatter | solution.py:13
  125.3 209.0 %reduce-scatter.5.cloned.1.call-start = ((), (), s32[]{:S(2)}) async-start(), calls=%async_computation.5 | async-start | bytes 4718592 | tf_op jit(solution)/shard_map/reduce_scatter | solution.py:13
Sparse Core Ops, SparseCore 0:
  9.2 96.4 all-gather.1
  125.4 151.1 reduce-scatter.2
  279.2 55.0 reduce-scatter.4
where the time goes:
time: 341 us
  waiting for transfers between devices  240 us (70%)
  blocking collectives  65.5 us (19%)
  matrix products  19.5 us (6%)
  between operations  13.1 us (4%)
    reduce_scatter x2, waiting for transfers between devices, sum_by_axis(): array = lax.psum_scatter(array, axis, scatter_dimension=dim, tiled=True)  209 us
    all_to_all x1, blocking collectives, local(): lax.all_to_all(cotangent, 'col', split_axis=1, concat_axis=0, tiled=True)  65.5 us
    all_gather x1, waiting for transfers between devices, local(): lax.all_gather(features, 'col', axis=0, tiled=True)  30.6 us
    dot_general x1, matrix products, tokens_product(): lax.dot_general(left, right, (((0,), (0,)), ((), ())), preferred_element_...  19.5 us
  transfers between devices with their start and end apart: 3, of which 3 were waited for; matrix products, arithmetic and copies ran while one was open for 1% of the time, Pallas kernels for 0%

commit v1 on v0

--- a/solution.py
+++ b/solution.py
@@ -22,7 +22,12 @@
 
 def local(features, cotangent):
     columns = lax.all_to_all(cotangent, "col", split_axis=1, concat_axis=0, tiled=True)
-    partial_value = tokens_product(lax.all_gather(features, "col", axis=0, tiled=True), columns)
+    partial_value = tokens_product(
+        jnp.concatenate(
+            lax.all_to_all(jnp.stack([features] * lax.axis_size("col")), "col", 0, 0), axis=0
+        ),
+        columns,
+    )
     return sum_by_axis(partial_value, ROW, 0)
 
 

time: 341 us -> 437 us (1.28)
  blocking collectives: 65.5 us -> 187 us
  waiting for transfers between devices: 240 us -> 211 us
  local copies, waits for them, and re-layouts: 2.32 us -> 9.88 us
    all_to_all x0 -> x1, blocking collectives: none -> 144 us  [local(): lax.all_to_all(jnp.stack([features] * lax.axis_size('col')), 'col', 0, 0)]
    all_gather x1 -> x0, waiting for transfers between devices: 30.6 us -> none  [local(): lax.all_gather(features, 'col', axis=0, tiled=True)]
    all_to_all x1, blocking collectives: 65.5 us -> 43.1 us  [local(): lax.all_to_all(cotangent, 'col', split_axis=1, concat_axis=0, tiled=True)]
    another operation x0 -> x1, local copies, waits for them, and re-layouts: none -> 7.56 us  [local(): jnp.stack([features] * lax.axis_size('col'))]
  transfers between devices with their start and end apart: 3 -> 2, of which waited for: 3 -> 2; matrix products, arithmetic and copies ran while one was open for 1% -> 0% of each run, Pallas kernels for 0% -> 0%
where the time goes in v1:
time: 437 us
  waiting for transfers between devices  211 us (48%)
  blocking collectives  187 us (43%)
  matrix products  16.2 us (4%)
  between operations  13.4 us (3%)
  local copies, waits for them, and re-layouts  9.88 us (2%)
    reduce_scatter x2, waiting for transfers between devices, sum_by_axis(): array = lax.psum_scatter(array, axis, scatter_dimension=dim, tiled=True)  211 us
    all_to_all x1, blocking collectives, local(): lax.all_to_all(jnp.stack([features] * lax.axis_size('col')), 'col', 0, 0)  144 us
    all_to_all x1, blocking collectives, local(): lax.all_to_all(cotangent, 'col', split_axis=1, concat_axis=0, tiled=True)  43.1 us
    dot_general x1, matrix products, tokens_product(): lax.dot_general(left, right, (((0,), (0,)), ((), ())), preferred_element_...  16.2 us
  transfers between devices with their start and end apart: 2, of which 2 were waited for; matrix products, arithmetic and copies ran while one was open for 0% of the time, Pallas kernels for 0%

profile of v1, /device:TPU:1, one launch (start us, length us, event | category | flops | bytes accessed | tf_op | source)
XLA Modules:
  0.0 436.9 jit_solution(16523650074647787561)
XLA Ops:
  6.5 0.0 reduce-scatter.3.cloned.1.call-start
  6.5 2.3 copy.6
  8.9 43.1 %all_to_all.21 = bf16[192,8,1024]{2,0,1:T(8,128)(2,1)S(1)} all-to-all(bf16[192,8,1024]{2,0,1:T(8,128)(2,1)S(1)} %bitcast.10), channel_id=1, replica_groups=mesh['row_0'=4,'row_1'=8,'col'=8] {'col'}, dimensions={1} | all-to-all | bytes 6291456 | tf_op jit(solution)/shard_map/all_to_all | solution.py:24
  51.9 7.6 %stack.2 = bf16[8,192,4096]{2,1,0:T(8,128)(2,1)} broadcast(bf16[192,4096]{1,0:T(8,128)(2,1)} %param.2), dimensions={1,2} | broadcast | bytes 14155776 | tf_op jit(solution)/shard_map/stack | solution.py:27
  59.5 143.5 %all_to_all.22 = bf16[8,192,4096]{2,1,0:T(8,128)(2,1)S(1)} all-to-all(bf16[8,192,4096]{2,1,0:T(8,128)(2,1)} %stack.2), channel_id=1, replica_groups=mesh['row_0'=4,'row_1'=8,'col'=8] {'col'}, dimensions={0} | all-to-all | bytes 25165824 | tf_op jit(solution)/shard_map/all_to_all | solution.py:27
  203.0 16.2 %convolution_bitcast_fusion = f32[4096,1024]{1,0:T(8,128)} fusion(bf16[8,192,4096]{2,1,0:T(8,128)(2,1)S(1)} %all_to_all.22, bf16[192,8,1024]{2,0,1:T(8,128)(2,1)S(1)} %all_to_all.21), kind=kOutput, calls=%fused_computation | convolution fusion | flops 12884901888 | bytes 32505856 | tf_op jit(solution)/shard_map/dot_general | solution.py:18
  219.2 0.0 reduce-scatter.3.cloned.1.call-update
  219.2 0.0 reduce-scatter.5.cloned.1.call-start
  219.3 153.2 %reduce-scatter.3.cloned.1.call-done = f32[1024,1024]{1,0:T(8,128)} async-done(((f32[4096,1024]{1,0:T(8,128)}), f32[1024,1024]{1,0:T(8,128)}) %reduce-scatter.3.cloned.1.call-update) | async-done | bytes 4194320 | tf_op jit(solution)/shard_map/reduce_scatter | solution.py:13
  372.5 0.0 reduce-scatter.5.cloned.1.call-update
  372.5 57.6 %reduce-scatter.5.cloned.1.call-done = f32[128,1024]{1,0:T(8,128)} async-done(((f32[1024,1024]{1,0:T(8,128)}), f32[128,1024]{1,0:T(8,128)}) %reduce-scatter.5.cloned.1.call-update) | async-done | bytes 524304 | tf_op jit(solution)/shard_map/reduce_scatter | solution.py:13
Async XLA Ops:
  6.5 365.9 %reduce-scatter.3.cloned.1.call-start = ((), (), s32[]{:S(2)}) async-start(), calls=%async_computation.4 | async-start | bytes 20971520 | tf_op jit(solution)/shard_map/reduce_scatter | solution.py:13
  219.2 210.8 %reduce-scatter.5.cloned.1.call-start = ((), (), s32[]{:S(2)}) async-start(), calls=%async_computation.5 | async-start | bytes 4718592 | tf_op jit(solution)/shard_map/reduce_scatter | solution.py:13
Sparse Core Ops, SparseCore 0:
  219.4 153.0 reduce-scatter.2
  375.0 55.0 reduce-scatter.4
